TPU v7x, 32 devices: a whole 2x2x4 slice. The times are simulated.
32 devices in a mesh: grp: 4 (over x, core), dp: 8 (over z, y).
Axes of the slice: x: 2, y: 2, z: 4, core: 2. Of those that a mesh axis runs over, the one named last changes fastest.
Arguments:
- gradients: bfloat16 [4, 8, 16384, 128], P('grp', 'dp'), may hold values from -48 to 48
- block_len: int32 [16], replicated, may hold values from 1 to 524288, 2097152 in all
- amax_history: float32 [4, 16], replicated, may hold values from 20 to 200
Outputs:
- mean_grad: bfloat16 [16384, 128], P('dp')
- block_amax: bfloat16 [16], replicated
Inputs may be any that keep to these rules, and one draw needn't show every extreme that they name: `block_len`: every tensor has at least one entry; the lengths sum to 2097152.
All inputs are finite; a program needn't handle non-finite values.
Results may differ from a plain program's by a relative error of at most 0.018.
Values may be sent and summed in bfloat16 or wider, within the bound.
A program may use at most 64 MiB of HBM per device.

v0:
```python
import functools

import jax
import jax.numpy as jnp
from jax import lax
from jax.experimental import pallas as pl
from jax.experimental.pallas import tpu as pltpu
from jax.sharding import PartitionSpec as P

SATURATE = 448.0
CHUNKS = 16
Z_FIRST = 3
STEP = 1
MESH = pl.DeviceIdType.MESH


def y_extent(dp):
    y = 1
    while (2 * y) * (2 * y) <= dp:
        y *= 2
    return y


def kernel(
    cfg, len_ref, hist_ref, grad, out, amax_out,
    own, ybuf, zin, zout, own_b, zin_b, zout_b, mout_b, yin_b,
    qbuf, scale_buf, svec, acc, msg, maxima,
    own_sem, y_send, y_recv, z_send, z_recv, q_send, q_recv,
    ob_sem, yb_send, yb_recv, zb_send, zb_recv, m_send, m_recv,
):
    dp, grp, Y, Z, K, NB, lines, piece = cfg
    NA = K - NB
    blocks = len_ref.shape[0]
    hist = hist_ref.shape[0]
    devices = dp * grp
    d = lax.axis_index("dp")
    g = lax.axis_index("grp")
    z, y = d // Y, d % Y
    base = d * (K * lines)

    def copy(src, dst, send, recv, target):
        return pltpu.make_async_remote_copy(
            src_ref=src, dst_ref=dst, send_sem=send, recv_sem=recv,
            device_id=target, device_id_type=MESH,
        )

    def own_copy(a):
        return pltpu.make_async_copy(grad.at[:, y, NB + a], own.at[a], own_sem.at[a])

    def own_b_copy(b):
        return pltpu.make_async_copy(grad.at[:, :, b], own_b.at[b], ob_sem.at[b])

    def y_copy(a, j):
        peer = (y + j) % Y
        return copy(grad.at[:, peer, NB + a], ybuf.at[a, j - 1], y_send.at[a, j - 1],
                    y_recv.at[a, j - 1], {"dp": z * Y + peer})

    def yb_copy(b, j):
        peer = (y + j) % Y
        return copy(mout_b.at[b, j - 1], yin_b.at[b, j - 1], yb_send.at[b, j - 1],
                    yb_recv.at[b, j - 1], {"dp": z * Y + peer})

    chain_a = (zin, zout, z_send, z_recv)
    chain_b = (zin_b, zout_b, zb_send, zb_recv)

    def hop(chain, i, way, t):
        into, outof, send, recv = chain
        return copy(outof.at[i, t], into.at[i, way, t], send.at[i, t], recv.at[i, way, t],
                    {"dp": (z + 1 - 2 * way) * Y + y})

    def arrival(chain, i, way, t):
        into, outof, send, recv = chain
        return copy(into.at[i, way, t], into.at[i, way, t], send.at[i, t], recv.at[i, way, t],
                    {"dp": (z - 1 + 2 * way) * Y + y})

    def await_hop(chain, i, way, t):
        @pl.when(z > 0 if way == 0 else z < Z - 1)
        def _():
            arrival(chain, i, way, t).wait_recv()

    def q_copy(k, j):
        return copy(qbuf.at[k, g], qbuf.at[k, g], q_send.at[k, j - 1], q_recv.at[k, j - 1],
                    {"grp": (g + j) % grp})

    def q_arrival(k, j):
        peer = (g + grp - j) % grp
        return copy(qbuf.at[k, peer], qbuf.at[k, peer], q_send.at[k, j - 1],
                    q_recv.at[k, j - 1], {"grp": peer})

    def device(j):
        flat = (d * grp + g + j) % devices
        return {"dp": flat // grp, "grp": flat % grp}

    def m_copy(j):
        return copy(msg, maxima.at[j - 1], m_send.at[j - 1], m_recv.at[j - 1], device(j))

    def every(action):
        def one(j, carry):
            action(j)
            return carry

        lax.fori_loop(1, devices, one, 0)

    barrier = pltpu.get_barrier_semaphore()
    every(lambda j: pl.semaphore_signal(
        barrier, inc=1, device_id=device(j), device_id_type=MESH))

    def each(count, action):
        def one(i, carry):
            action(i)
            return carry

        lax.fori_loop(0, count, one, 0)

    def upto(limit, action):
        for i in range(Z - 1):
            pl.when(limit > i)(functools.partial(action, i))

    each(NB, lambda b: own_b_copy(b).start())
    each(NA, lambda a: own_copy(a).start())
    for way, end in ((0, 0), (1, Z - 1)):
        @pl.when(z == end)
        def _(way=way):
            def clear(chain):
                into = chain[0]

                def one(i):
                    into[i, way] = jnp.zeros(into.shape[2:], into.dtype)

                return one

            each(NA, clear(chain_a))
            each(NB, clear(chain_b))
    ends = []
    total = jnp.int32(0)
    for c in range(blocks):
        total = total + len_ref[c]
        ends.append(total)
        top = jnp.full((8, 128), hist_ref[0, c], jnp.float32)
        for h in range(1, hist):
            top = jnp.maximum(top, jnp.full((8, 128), hist_ref[h, c], jnp.float32))
        svec[c] = SATURATE / jnp.maximum(top, 1.0)
    acc[...] = jnp.zeros(acc.shape, jnp.float32)
    pl.semaphore_wait(barrier, devices - 1)

    def send_y(a):
        for j in range(1, Y):
            y_copy(a, j).start()

    each(NA, send_y)

    def term_a(a, t):
        value = own[a, t].astype(jnp.float32)
        for i in range(Y - 1):
            value = value + ybuf[a, i, t].astype(jnp.float32)
        return value

    def term_b(b, t):
        return own_b[b, t].astype(jnp.float32)

    def stage_y(a):
        own_copy(a).wait()
        for j in range(1, Y):
            y_copy(a, j).wait_recv()

    def pass_on(chain, term, i, way):
        def one(s):
            t = Z - 1 - s if way == 0 else s
            await_hop(chain, i, way, t)
            value = term(i, t) + chain[0][i, way, t].astype(jnp.float32)
            chain[1][i, t] = value.astype(jnp.bfloat16)
            hop(chain, i, way, t).start()

        upto(Z - 1 - z if way == 0 else z, one)

    def merge_b(b):
        for way in range(2):
            await_hop(chain_b, b, way, z)
        for j in range(1, Y):
            peer = (y + j) % Y
            value = own_b[b, z, peer].astype(jnp.float32)
            for way in range(2):
                value = value + zin_b[b, way, z, peer].astype(jnp.float32)
            mout_b[b, j - 1] = value.astype(jnp.bfloat16)
            yb_copy(b, j).start()

    def q_a(a):
        for way in range(2):
            await_hop(chain_a, a, way, z)

        def total(rows):
            value = own[a, z, rows].astype(jnp.float32)
            for i in range(Y - 1):
                value = value + ybuf[a, i, z, rows].astype(jnp.float32)
            for way in range(2):
                value = value + zin[a, way, z, rows].astype(jnp.float32)
            return value

        stage_q(NB + a, total)

    def q_b(b):
        for j in range(1, Y):
            yb_copy(b, j).wait_recv()

        def total(rows):
            value = own_b[b, z, y, rows].astype(jnp.float32)
            for way in range(2):
                value = value + zin_b[b, way, z, y, rows].astype(jnp.float32)
            for i in range(Y - 1):
                value = value + yin_b[b, i, rows].astype(jnp.float32)
            return value

        stage_q(b, total)

    def stage_q(k, total):
        def step(i, tops):
            rows = pl.ds(pl.multiple_of(i * piece, piece), piece)
            value = total(rows)
            value = value.reshape(piece // 8, 8, 128)
            shape = value.shape
            first = (base + k * lines + i * piece) * 128
            place = (
                lax.broadcasted_iota(jnp.int32, shape, 0) * 1024
                + lax.broadcasted_iota(jnp.int32, shape, 1) * 128
                + lax.broadcasted_iota(jnp.int32, shape, 2)
            ) + first
            size = jnp.abs(value)
            scale = jnp.broadcast_to(svec[0][None], shape)
            below = place < ends[0]
            new = [jnp.maximum(tops[0], jnp.max(jnp.where(below, size, 0.0), axis=0))]
            for c in range(1, blocks):
                after = place >= ends[c - 1]
                scale = jnp.where(after, svec[c][None], scale)
                inside = after & (place < ends[c])
                new.append(jnp.maximum(tops[c], jnp.max(jnp.where(inside, size, 0.0), axis=0)))
            scale_buf[k, rows] = scale.reshape(piece, 128)
            quant = jnp.clip(value * scale, -SATURATE, SATURATE)
            qbuf[k, g, rows] = quant.reshape(piece, 128).astype(jnp.bfloat16)
            return tuple(new)

        tops = lax.fori_loop(0, lines // piece, step, tuple(acc[c] for c in range(blocks)))
        for c in range(blocks):
            acc[c] = tops[c]
        for j in range(1, grp):
            q_copy(k, j).start()

    def stage_max():
        top = jnp.max(acc[...], axis=1)
        top = jnp.max(top, axis=1, keepdims=True)
        lane = lax.broadcasted_iota(jnp.int32, (blocks, 128), 1)
        row = lax.broadcasted_iota(jnp.int32, (blocks, 128), 0)
        flat = jnp.max(jnp.where(lane == row, top, 0.0), axis=0, keepdims=True)
        msg[...] = flat
        every(lambda j: m_copy(j).start())

    def stage_out(k):
        for j in range(1, grp):
            q_arrival(k, j).wait_recv()
        value = qbuf[k, 0].astype(jnp.float32)
        for a in range(1, grp):
            value = value + qbuf[k, a].astype(jnp.float32)
        out[k] = (value / scale_buf[k] / (dp * grp)).astype(jnp.bfloat16)

    reach = STEP * (Z - 1)
    last = K + reach
    stages = (
        (lambda b: own_b_copy(b).wait(), NB, 0),
        (lambda b: pass_on(chain_b, term_b, b, 0), NB, STEP * z),
        (lambda b: pass_on(chain_b, term_b, b, 1), NB, STEP * (Z - 1 - z)),
        (merge_b, NB, reach + 1),
        (stage_y, NA, NB),
        (lambda a: pass_on(chain_a, term_a, a, 0), NA, NB + STEP * z),
        (lambda a: pass_on(chain_a, term_a, a, 1), NA, NB + STEP * (Z - 1 - z)),
        (q_b, NB, K),
        (q_a, NA, NB + reach + 1),
        (lambda b: stage_out(b), NB, K + 3),
        (lambda a: stage_out(NB + a), NA, NB + reach + 4),
    )

    def tick(t, carry):
        for stage, count, delay in stages:
            @pl.when((t >= delay) & (t < count + delay))
            def _(stage=stage, delay=delay):
                stage(t - delay)

            if stage is q_a:
                @pl.when(t == last)
                def _():
                    stage_max()
        return carry

    lax.fori_loop(0, K + reach + 4, tick, 0)

    every(lambda j: m_copy(j).wait_recv())
    top = jnp.maximum(jnp.max(maxima[...], axis=0), msg[...])
    amax_out[...] = jnp.broadcast_to(top, amax_out.shape).astype(jnp.bfloat16)

    def finish_a(a):
        for j in range(1, Y):
            y_copy(a, j).wait_send()
        upto(Z - 1 - z, lambda s: hop(chain_a, a, 0, Z - 1 - s).wait_send())
        upto(z, lambda s: hop(chain_a, a, 1, s).wait_send())

    def finish_b(b):
        for j in range(1, Y):
            yb_copy(b, j).wait_send()
        upto(Z - 1 - z, lambda s: hop(chain_b, b, 0, Z - 1 - s).wait_send())
        upto(z, lambda s: hop(chain_b, b, 1, s).wait_send())

    def finish(k):
        for j in range(1, grp):
            q_copy(k, j).wait_send()

    each(NA, finish_a)
    each(NB, finish_b)
    each(K, finish)
    every(lambda j: m_copy(j).wait_send())


def body(gradients, block_len, amax_history):
    dp = lax.axis_size("dp")
    grp = lax.axis_size("grp")
    rows, lanes = gradients.shape[2:]
    Y = y_extent(dp)
    Z = dp // Y
    K = min(CHUNKS, rows // dp // 32)
    NB = min(Z_FIRST, K - 1)
    NA = K - NB
    lines = rows // dp // K
    piece = 32
    blocks = block_len.shape[0]
    cfg = (dp, grp, Y, Z, K, NB, lines, piece)
    bf, f32 = jnp.bfloat16, jnp.float32
    sem = pltpu.SemaphoreType.DMA
    tile = (lines, lanes)
    scratch = [
        pltpu.VMEM((NA, Z) + tile, bf),
        pltpu.VMEM((NA, Y - 1, Z) + tile, bf),
        pltpu.VMEM((NA, 2, Z) + tile, bf),
        pltpu.VMEM((NA, Z) + tile, bf),
        pltpu.VMEM((NB, Z, Y) + tile, bf),
        pltpu.VMEM((NB, 2, Z, Y) + tile, bf),
        pltpu.VMEM((NB, Z, Y) + tile, bf),
        pltpu.VMEM((NB, Y - 1) + tile, bf),
        pltpu.VMEM((NB, Y - 1) + tile, bf),
        pltpu.VMEM((K, grp) + tile, bf),
        pltpu.VMEM((K,) + tile, f32),
        pltpu.VMEM((blocks, 8, lanes), f32),
        pltpu.VMEM((blocks, 8, lanes), f32),
        pltpu.VMEM((1, lanes), f32),
        pltpu.VMEM((dp * grp - 1, 1, lanes), f32),
        sem((NA,)),
        sem((NA, Y - 1)), sem((NA, Y - 1)),
        sem((NA, Z)), sem((NA, 2, Z)),
        sem((K, grp - 1)), sem((K, grp - 1)),
        sem((NB,)),
        sem((NB, Y - 1)), sem((NB, Y - 1)),
        sem((NB, Z)), sem((NB, 2, Z)),
        sem((dp * grp - 1,)), sem((dp * grp - 1,)),
    ]
    mean, top = pl.pallas_call(
        functools.partial(kernel, cfg),
        out_shape=(
            jax.ShapeDtypeStruct((K,) + tile, bf),
            jax.ShapeDtypeStruct((8, lanes), bf),
        ),
        in_specs=[
            pl.BlockSpec(memory_space=pltpu.SMEM),
            pl.BlockSpec(memory_space=pltpu.SMEM),
            pl.BlockSpec(memory_space=pltpu.HBM),
        ],
        out_specs=(
            pl.BlockSpec(memory_space=pltpu.VMEM),
            pl.BlockSpec(memory_space=pltpu.VMEM),
        ),
        scratch_shapes=scratch,
        compiler_params=pltpu.CompilerParams(collective_id=0, has_side_effects=True),
    )(block_len, amax_history, gradients.reshape((Z, Y, K) + tile))
    return mean.reshape(rows // dp, lanes), top[0, :blocks]


def solution(mesh):
    placed = (P("grp", "dp", None, None), P(), P())
    return jax.shard_map(
        body, mesh=mesh, in_specs=placed, out_specs=(P("dp", None), P()), check_vma=False
    )
```

profile of v0, /device:TPU:0, one launch (start us, length us, event | category | flops | bytes accessed | tf_op | source)
XLA Modules:
  0.0 69.0 jit_solution(11665397547488170121)
XLA Ops:
  0.6 65.3 %shard_map.50 = (bf16[16,128,128]{2,1,0:T(8,128)(2,1)}, bf16[8,128]{1,0:T(8,128)(2,1)}) custom-call(s32[16]{0:T(128)} %len_ref.1, f32[4,16]{1,0:T(4,128)} %hist_ref.1, bf16[4,2,16,128,128]{4,3,2,1,0:T(8,128)(2,1)} %bitcast.4), custom_call_target="tpu_custom_call" | custom-call | tf_op jit(solution)/shard_map/pallas_call | solution.py:361
  65.9 1.2 %slice_bitcast_fusion = bf16[16]{0:T(256)(128)(2,1)} fusion(bf16[8,128]{1,0:T(8,128)(2,1)} %get-tuple-element.5), kind=kLoop, calls=%fused_computation | loop fusion | bytes 64 | tf_op jit(solution)/shard_map/squeeze | solution.py:379
  67.1 1.9 %copy.6 = bf16[2048,128]{1,0:T(8,128)(2,1)} copy(bf16[2048,128]{1,0:T(8,128)(2,1)} %bitcast.5) | data formatting | bytes 1048576
where the time goes:
time: 69.2 us; the launch traced here: 69 us
  Pallas kernels  65.3 us (94%)
  local copies, waits for them, and re-layouts  3.05 us (4%)
    pallas_call x1, Pallas kernels, body(): pl.pallas_call(functools.partial(kernel, cfg), out_shape=(jax.ShapeDtypeS...  65.3 us
    unnamed x1, local copies, waits for them, and re-layouts  1.87 us

commit v1 on v0

v1 whole, which is shorter than its diff:
```python
import functools

import jax
import jax.numpy as jnp
from jax import lax
from jax.experimental import pallas as pl
from jax.experimental.pallas import tpu as pltpu
from jax.sharding import PartitionSpec as P

SATURATE = 448.0
CHUNKS = 16
CORES = 2
LAG_PAIR = 2
LAG_MEAN = 5
LAG_BACK = 7
MESH = pl.DeviceIdType.MESH


def y_extent(dp):
    y = 1
    while (2 * y) * (2 * y) <= dp:
        y *= 2
    return y


def kernel(
    cfg, len_hbm, hist_hbm, grad, out, amax_out,
    len_ref, hist_ref, own, ring, qown, qsib, pair, xbuf, fin_out, fin_in,
    scale_buf, inv_buf, block_buf, acc, msg, maxima,
    small_sem, own_sem, r_send, r_recv, q_send, q_recv, x_send, x_recv,
    f_send, f_recv, m_send, m_recv,
):
    N, grp, Y, Z, K, lines, piece = cfg
    far = N // 2
    X = grp // CORES
    half = lines // CORES
    blocks = len_ref.shape[0]
    hist = hist_ref.shape[0]
    devices = N * grp
    d = lax.axis_index("dp")
    g = lax.axis_index("grp")
    core = g % CORES
    bf, f32 = jnp.bfloat16, jnp.float32

    snake = Y * (Z - 1)

    def place_of(d):
        z, y = d // Y, d % Y
        up = (z + Z - 1) // Z
        odd = y % 2
        along = (z - 1) * (1 - odd) + (Z - 1 - z) * odd
        return up * (y * (Z - 1) + along) + (1 - up) * (snake + Y - 1 - y)

    def device_at(p):
        p = p % N
        back = p // snake
        y = p // (Z - 1)
        r = p % (Z - 1)
        odd = y % 2
        z = 1 + r * (1 - odd) + (Z - 2 - r) * odd
        return (1 - back) * (z * Y + y) + back * (Y - 1 - (p - snake))

    me = place_of(d)
    ahead = (device_at(me + 1), device_at(me + N - 1))

    def slice_at(way, dist):
        return device_at(me + (dist if way == 0 else N - dist))

    def remote(src, dst, send, recv, target):
        return pltpu.make_async_remote_copy(
            src_ref=src, dst_ref=dst, send_sem=send, recv_sem=recv,
            device_id=target, device_id_type=MESH,
        )

    def own_copy(s):
        return pltpu.make_async_copy(grad.at[s], own.at[s], own_sem.at[s])

    def first_hop(way, dist, k):
        return remote(grad.at[slice_at(way, dist), k], ring.at[way, dist - 1, k],
                      r_send.at[k], r_recv.at[way, dist - 1, k], {"dp": ahead[way]})

    def next_hop(way, dist, k):
        return remote(ring.at[way, dist, k], ring.at[way, dist - 1, k],
                      r_send.at[k], r_recv.at[way, dist - 1, k], {"dp": ahead[way]})

    def await_ring(way, dist, k):
        remote(ring.at[way, dist, k], ring.at[way, dist, k], r_send.at[k],
               r_recv.at[way, dist, k], {"dp": ahead[1 - way]}).wait_recv()

    def relay(way, dist, k):
        await_ring(way, dist, k)
        ring[way, dist, k] = ring[way, dist, k] + own[slice_at(way, dist), k]
        next_hop(way, dist, k).start()

    mine = pl.ds(pl.multiple_of(core * half, half), half)
    theirs = pl.ds(pl.multiple_of((CORES - 1 - core) * half, half), half)
    sibling = {"grp": g + CORES - 1 - 2 * core}

    def q_copy(k):
        return remote(qown.at[k, theirs], qsib.at[k], q_send, q_recv.at[k], sibling)

    def x_peer(j):
        return {"grp": (g + CORES * j) % grp}

    def x_copy(k, j):
        return remote(pair.at[k], xbuf.at[k, j - 1], x_send, x_recv.at[k, j - 1], x_peer(j))

    def f_copy(k):
        return remote(fin_out.at[k], fin_in.at[k], f_send, f_recv.at[k], sibling)

    def device(j):
        flat = (d * grp + g + j) % devices
        return {"dp": flat // grp, "grp": flat % grp}

    def m_copy(j):
        return remote(msg, maxima.at[j - 1], m_send, m_recv, device(j))

    def drain(ref, sem):
        pltpu.make_async_copy(ref, ref, sem).wait()

    def each(lower, upper, action):
        def one(i, carry):
            action(i)
            return carry

        lax.fori_loop(lower, upper, one, 0)

    barrier = pltpu.get_barrier_semaphore()
    near = [{"dp": ahead[0]}, {"dp": ahead[1]}, sibling]
    near += [x_peer(j) for j in range(1, X)]
    for target in near:
        pl.semaphore_signal(barrier, inc=1, device_id=target, device_id_type=MESH)
    len_copy = pltpu.make_async_copy(len_hbm, len_ref, small_sem.at[0])
    hist_copy = pltpu.make_async_copy(hist_hbm, hist_ref, small_sem.at[1])
    len_copy.start()
    hist_copy.start()
    each(0, N, lambda s: own_copy(s).start())
    pl.semaphore_wait(barrier, len(near))

    def start_far(m):
        first_hop(0, far, 2 * m).start()
        first_hop(1, far, 2 * m + 1).start()

    each(0, K // 2, start_far)

    acc[...] = jnp.zeros(acc.shape, f32)
    len_copy.wait()
    hist_copy.wait()
    ends = []
    factors = []
    total = jnp.int32(0)
    for c in range(blocks):
        total = total + len_ref[c]
        ends.append(total)
        top = hist_ref[0, c]
        for h in range(1, hist):
            top = jnp.maximum(top, hist_ref[h, c])
        top = jnp.maximum(jnp.full((8, 128), top, f32), 1.0)
        factors.append((SATURATE / top, top * (1.0 / (SATURATE * devices))))

    each(0, N, lambda s: own_copy(s).wait())

    def second(m):
        if far > 1:
            relay(0, far - 1, 2 * m)
            first_hop(1, far - 1, 2 * m).start()
            first_hop(0, far - 1, 2 * m + 1).start()
            relay(1, far - 1, 2 * m + 1)

    each(0, K // 2, second)

    def prepare(i):
        shape = (piece // 8, 8, 128)
        at = (
            lax.broadcasted_iota(jnp.int32, shape, 0) * 1024
            + lax.broadcasted_iota(jnp.int32, shape, 1) * 128
            + lax.broadcasted_iota(jnp.int32, shape, 2)
        ) + (d * (K * lines) + i * piece) * 128
        block = jnp.zeros(shape, jnp.int32)
        scale = jnp.broadcast_to(factors[0][0][None], shape)
        inv = jnp.broadcast_to(factors[0][1][None], shape)
        for c in range(1, blocks):
            after = at >= ends[c - 1]
            block = jnp.where(after, c, block)
            scale = jnp.where(after, factors[c][0][None], scale)
            inv = jnp.where(after, factors[c][1][None], inv)
        rows = pl.ds(pl.multiple_of(i * piece, piece), piece)
        block_buf[rows] = block.reshape(piece, 128)
        scale_buf[rows] = scale.reshape(piece, 128)
        inv_buf[rows] = inv.reshape(piece, 128)

    each(0, K * lines // piece, prepare)

    def phase(h, carry):
        dist = far - h

        def one(k, carry):
            relay(0, dist, k)
            relay(1, dist, k)
            return carry

        return lax.fori_loop(0, K, one, carry)

    lax.fori_loop(2, far, phase, 0)

    def stage_q(k):
        await_ring(0, 0, k)
        await_ring(1, 0, k)

        def step(i, tops):
            rows = pl.ds(pl.multiple_of(i * piece, piece), piece)
            flat = pl.ds(pl.multiple_of(k * lines + i * piece, piece), piece)
            value = own[d, k, rows].astype(f32)
            value = value + ring[0, 0, k, rows].astype(f32) + ring[1, 0, k, rows].astype(f32)
            quant = jnp.clip(value * scale_buf[flat], -SATURATE, SATURATE)
            qown[k, rows] = quant.astype(bf)
            size = jnp.abs(value).reshape(piece // 8, 8, 128)
            block = block_buf[flat].reshape(piece // 8, 8, 128)
            return tuple(
                jnp.maximum(tops[c], jnp.max(jnp.where(block == c, size, 0.0), axis=0))
                for c in range(blocks)
            )

        tops = lax.fori_loop(0, lines // piece, step, tuple(acc[c] for c in range(blocks)))
        q_copy(k).start()
        for c in range(blocks):
            acc[c] = tops[c]

    def stage_pair(k):
        q_copy(k).wait_recv()
        pair[k] = (qown[k, mine].astype(f32) + qsib[k].astype(f32)).astype(bf)
        for j in range(1, X):
            x_copy(k, j).start()

    def stage_mean(k):
        value = pair[k].astype(f32)
        for j in range(1, X):
            x_copy(k, j).wait_recv()
            value = value + xbuf[k, j - 1].astype(f32)
        rows = pl.ds(pl.multiple_of(k * lines + core * half, half), half)
        mean = (value * inv_buf[rows]).astype(bf)
        out[k, mine] = mean
        fin_out[k] = mean
        f_copy(k).start()

    def stage_back(k):
        f_copy(k).wait_recv()
        out[k, theirs] = fin_in[k]

    def stage_max():
        top = jnp.max(acc[...], axis=1)
        top = jnp.max(top, axis=1, keepdims=True)
        lane = lax.broadcasted_iota(jnp.int32, (blocks, 128), 1)
        row = lax.broadcasted_iota(jnp.int32, (blocks, 128), 0)
        msg[...] = jnp.max(jnp.where(lane == row, top, 0.0), axis=0, keepdims=True)
        each(1, devices, lambda j: m_copy(j).start())

    def tick(t, carry):
        @pl.when(t < K)
        def _():
            stage_q(t)

        @pl.when(t == K - 1)
        def _():
            stage_max()

        @pl.when((t >= LAG_PAIR) & (t < K + LAG_PAIR))
        def _():
            stage_pair(t - LAG_PAIR)

        @pl.when((t >= LAG_MEAN) & (t < K + LAG_MEAN))
        def _():
            stage_mean(t - LAG_MEAN)

        @pl.when(t >= LAG_BACK)
        def _():
            k = t - LAG_BACK
            stage_back(k)
            drain(own.at[pl.ds(0, N - 1), k], r_send.at[k])

        return carry

    lax.fori_loop(0, K + LAG_BACK, tick, 0)

    drain(maxima, m_recv)
    top = jnp.maximum(jnp.max(maxima[...], axis=0), msg[...])
    amax_out[...] = jnp.broadcast_to(top, amax_out.shape).astype(bf)
    drain(maxima, m_send)
    drain(qsib, q_send)
    drain(xbuf, x_send)
    drain(fin_in, f_send)


def body(gradients, block_len, amax_history):
    dp = lax.axis_size("dp")
    grp = lax.axis_size("grp")
    rows, lanes = gradients.shape[2:]
    Y = y_extent(dp)
    Z = dp // Y
    K = min(CHUNKS, rows // dp // 32)
    lines = rows // dp // K
    half = lines // CORES
    piece = min(32, lines)
    far = dp // 2
    X = grp // CORES
    cfg = (dp, grp, Y, Z, K, lines, piece)
    bf, f32 = jnp.bfloat16, jnp.float32
    dma = pltpu.SemaphoreType.DMA
    tile = (lines, lanes)
    part = (half, lanes)
    scratch = [
        pltpu.SMEM(block_len.shape, jnp.int32),
        pltpu.SMEM(amax_history.shape, f32),
        pltpu.VMEM((dp, K) + tile, bf),
        pltpu.VMEM((2, far, K) + tile, bf),
        pltpu.VMEM((K,) + tile, bf),
        pltpu.VMEM((K,) + part, bf),
        pltpu.VMEM((K,) + part, bf),
        pltpu.VMEM((K, X - 1) + part, bf),
        pltpu.VMEM((K,) + part, bf),
        pltpu.VMEM((K,) + part, bf),
        pltpu.VMEM((rows // dp, lanes), f32),
        pltpu.VMEM((rows // dp, lanes), f32),
        pltpu.VMEM((rows // dp, lanes), jnp.int32),
        pltpu.VMEM((block_len.shape[0], 8, lanes), f32),
        pltpu.VMEM((1, lanes), f32),
        pltpu.VMEM((dp * grp - 1, 1, lanes), f32),
        dma((2,)),
        dma((dp,)),
        dma((K,)), dma((2, far, K)),
        dma(()), dma((K,)),
        dma(()), dma((K, X - 1)),
        dma(()), dma((K,)),
        dma(()), dma(()),
    ]
    hbm = pl.BlockSpec(memory_space=pltpu.HBM)
    vmem = pl.BlockSpec(memory_space=pltpu.VMEM)
    pinned = [
        pltpu.with_memory_space_constraint(a, pltpu.HBM)
        for a in (block_len, amax_history, gradients.reshape((dp, K) + tile))
    ]
    mean, top = pl.pallas_call(
        functools.partial(kernel, cfg),
        out_shape=(
            jax.ShapeDtypeStruct((K,) + tile, bf),
            jax.ShapeDtypeStruct((8, lanes), bf),
        ),
        in_specs=[hbm, hbm, hbm],
        out_specs=(vmem, vmem),
        scratch_shapes=scratch,
        compiler_params=pltpu.CompilerParams(
            collective_id=0, has_side_effects=True, vmem_limit_bytes=24 << 20
        ),
    )(*pinned)
    return mean.reshape(rows // dp, lanes), top[0, : block_len.shape[0]]


def solution(mesh):
    placed = (P("grp", "dp", None, None), P(), P())
    return jax.shard_map(
        body, mesh=mesh, in_specs=placed, out_specs=(P("dp", None), P()), check_vma=False
    )
```

time: 69.2 us -> 56.1 us (0.81)
  Pallas kernels: 65.3 us -> 54 us
  local copies, waits for them, and re-layouts: 3.05 us -> 1.31 us
    pallas_call x1, Pallas kernels: 65.3 us -> 54 us  [body(): pl.pallas_call(functools.partial(kernel, cfg), out_shape=(jax.ShapeDtypeS...]
    unnamed x1, local copies, waits for them, and re-layouts: 1.87 us -> 0.79 us
where the time goes in v1:
time: 56.1 us; the launch traced here: 56 us
  Pallas kernels  54 us (96%)
  local copies, waits for them, and re-layouts  1.31 us (2%)
  between operations  0.64 us (1%)
    pallas_call x1, Pallas kernels, body(): pl.pallas_call(functools.partial(kernel, cfg), out_shape=(jax.ShapeDtypeS...  54 us

profile of v1, /device:TPU:0, one launch (start us, length us, event | category | flops | bytes accessed | tf_op | source)
XLA Modules:
  0.0 56.0 jit_solution(1606963466729064563)
XLA Ops:
  0.6 54.0 %shard_map.50 = (bf16[16,128,128]{2,1,0:T(8,128)(2,1)S(1)}, bf16[8,128]{1,0:T(8,128)(2,1)S(1)}) custom-call(s32[16]{0:T(128)} %len_hbm.1, f32[4,16]{1,0:T(4,128)} %hist_hbm.1, bf16[8,16,128,128]{3,2,1,0:T(8,128)(2,1)} %bitcast.5), custom_call_target="tpu_custom_call" | custom-call | tf_op jit(solution)/shard_map/pallas_call | solution.py:342
  54.7 0.5 slice_bitcast_fusion
  55.2 0.8 %copy.6 = bf16[2048,128]{1,0:T(8,128)(2,1)} copy(bf16[2048,128]{1,0:T(8,128)(2,1)S(1)} %bitcast.4) | data formatting | bytes 1048576

commit v2 on v1

v2 whole, which is shorter than its diff:
```python
import functools

import jax
import jax.numpy as jnp
from jax import lax
from jax.experimental import pallas as pl
from jax.experimental.pallas import tpu as pltpu
from jax.sharding import PartitionSpec as P

SATURATE = 448.0
CHUNKS = 4
SPLIT = 4
DIRECT = 1
CORES = 2
LAG_PAIR = 2
LAG_MEAN = 7
LAG_BACK = 9
MESH = pl.DeviceIdType.MESH


def y_extent(dp):
    y = 1
    while (2 * y) * (2 * y) <= dp:
        y *= 2
    return y


def kernel(
    cfg, len_hbm, hist_hbm, grad, out, amax_out,
    len_ref, hist_ref, own, ring, qown, qsib, pair, qall, fin_out, fin_in,
    scale_buf, inv_buf, block_buf, acc, msg, maxima,
    small_sem, own_sem, r_send, r_recv, e_recv, q_send, q_recv, x_send, x_recv,
    f_send, f_recv, d_send, d_recv, m_send, m_recv,
):
    N, grp, Y, Z, K, S, D, lines, piece = cfg
    far = N // 2
    X = grp // CORES
    sub = lines // S
    T = K * S
    half = sub // CORES
    blocks = len_ref.shape[0]
    hist = hist_ref.shape[0]
    devices = N * grp
    d = lax.axis_index("dp")
    g = lax.axis_index("grp")
    core = g % CORES
    bf, f32 = jnp.bfloat16, jnp.float32

    snake = Y * (Z - 1)

    def place_of(d):
        z, y = d // Y, d % Y
        up = (z + Z - 1) // Z
        odd = y % 2
        along = (z - 1) * (1 - odd) + (Z - 1 - z) * odd
        return up * (y * (Z - 1) + along) + (1 - up) * (snake + Y - 1 - y)

    def device_at(p):
        p = p % N
        back = p // snake
        y = p // (Z - 1)
        r = p % (Z - 1)
        odd = y % 2
        z = 1 + r * (1 - odd) + (Z - 2 - r) * odd
        return (1 - back) * (z * Y + y) + back * (Y - 1 - (p - snake))

    me = place_of(d)
    ahead = (device_at(me + 1), device_at(me + N - 1))
    sibling = {"grp": g + CORES - 1 - 2 * core}

    def peer(j):
        return {"grp": (g + j) % grp}

    barrier = pltpu.get_barrier_semaphore()
    near = [{"dp": ahead[0]}, {"dp": ahead[1]}]
    near += [peer(j) for j in range(1, grp)]
    for target in near:
        pl.semaphore_signal(barrier, inc=1, device_id=target, device_id_type=MESH)

    def slice_at(way, dist):
        return device_at(me + (dist if way == 0 else N - dist))

    def span(i, size):
        return pl.ds(pl.multiple_of(i * size, size), size)

    def remote(src, dst, send, recv, target):
        return pltpu.make_async_remote_copy(
            src_ref=src, dst_ref=dst, send_sem=send, recv_sem=recv,
            device_id=target, device_id_type=MESH,
        )

    def own_copy(s):
        return pltpu.make_async_copy(grad.at[s], own.at[s], own_sem.at[s])

    def hop(way, dist, k, src):
        rows = span(k, lines)
        return remote(src.at[rows], ring.at[way, dist - 1, rows], r_send.at[k],
                      r_recv.at[way, dist - 1, k], {"dp": ahead[way]})

    def end_hop(way, t, k, src):
        rows = span(t, sub)
        return remote(src.at[rows], ring.at[way, 0, rows], r_send.at[k],
                      e_recv.at[way, t], {"dp": ahead[way]})

    def await_hop(way, dist, k):
        rows = span(k, lines)
        here = ring.at[way, dist, rows]
        remote(here, here, r_send.at[k], r_recv.at[way, dist, k],
               {"dp": ahead[1 - way]}).wait_recv()

    def await_end(way, t):
        here = ring.at[way, 0, span(t, sub)]
        remote(here, here, r_send.at[t // S], e_recv.at[way, t],
               {"dp": ahead[1 - way]}).wait_recv()

    def first(way, dist, k):
        src = grad.at[slice_at(way, dist)]
        if dist > 1:
            hop(way, dist, k, src).start()
        else:
            for s in range(S):
                end_hop(way, k * S + s, k, src).start()

    def relay(way, dist, k):
        await_hop(way, dist, k)
        rows = span(k, lines)
        ring[way, dist, rows] = ring[way, dist, rows] + own[slice_at(way, dist), rows]
        hop(way, dist, k, ring.at[way, dist]).start()

    def end_relay(way, k):
        await_hop(way, 1, k)
        for s in range(S):
            t = k * S + s
            rows = span(t, sub)
            ring[way, 1, rows] = ring[way, 1, rows] + own[slice_at(way, 1), rows]
            end_hop(way, t, k, ring.at[way, 1]).start()

    def mine(t):
        return pl.ds(pl.multiple_of(t * sub + core * half, half), half)

    def theirs(t):
        return pl.ds(pl.multiple_of(t * sub + (CORES - 1 - core) * half, half), half)

    def q_copy(t):
        return remote(qown.at[theirs(t)], qsib.at[t], q_send, q_recv.at[t], sibling)

    x = g // CORES

    def x_copy(t, j):
        return remote(pair.at[t, x], pair.at[t, x], x_send, x_recv.at[t, j - 1], peer(CORES * j))

    def x_arrival(t, j):
        here = pair.at[t, (x + X - j) % X]
        return remote(here, here, x_send, x_recv.at[t, j - 1], peer(grp - CORES * j))

    def f_copy(t):
        return remote(fin_out.at[t], fin_in.at[t], f_send, f_recv.at[t], sibling)

    def d_copy(t, j):
        i = t - (T - D)
        return remote(qall.at[i, g], qall.at[i, g], d_send, d_recv.at[i, j - 1], peer(j))

    def d_arrival(t, j):
        i = t - (T - D)
        here = qall.at[i, (g + grp - j) % grp]
        return remote(here, here, d_send, d_recv.at[i, j - 1], peer(grp - j))

    def m_copy(j):
        flat = d * grp + g
        to = j + (j - flat + devices) // devices
        slot = flat - (flat - to - 1 + devices) // devices
        return remote(msg, maxima.at[slot], m_send, m_recv,
                      {"dp": to // grp, "grp": to % grp})

    def drain(ref, sem):
        pltpu.make_async_copy(ref, ref, sem).wait()

    def each(lower, upper, action):
        def one(i, carry):
            action(i)
            return carry

        lax.fori_loop(lower, upper, one, 0)

    pl.semaphore_wait(barrier, len(near))

    def start_far(m):
        first(0, far, 2 * m)
        first(1, far, 2 * m + 1)

    each(0, K // 2, start_far)

    len_copy = pltpu.make_async_copy(len_hbm, len_ref, small_sem.at[0])
    hist_copy = pltpu.make_async_copy(hist_hbm, hist_ref, small_sem.at[1])
    len_copy.start()
    hist_copy.start()
    each(0, N, lambda s: own_copy(s).start())
    acc[...] = jnp.zeros(acc.shape, f32)
    len_copy.wait()
    hist_copy.wait()
    ends = []
    factors = []
    total = jnp.int32(0)
    for c in range(blocks):
        total = total + len_ref[c]
        ends.append(total)
        top = hist_ref[0, c]
        for h in range(1, hist):
            top = jnp.maximum(top, hist_ref[h, c])
        top = jnp.maximum(jnp.full((8, 128), top, f32), 1.0)
        factors.append((SATURATE / top, top * (1.0 / (SATURATE * devices))))

    each(0, N, lambda s: own_copy(s).wait())

    def pass_on(way, dist, k):
        if dist == 1:
            end_relay(way, k)
        else:
            relay(way, dist, k)

    def second(m):
        pass_on(0, far - 1, 2 * m)
        first(1, far - 1, 2 * m)
        first(0, far - 1, 2 * m + 1)
        pass_on(1, far - 1, 2 * m + 1)

    each(0, K // 2, second)

    def prepare(i):
        shape = (piece // 8, 8, 128)
        at = (
            lax.broadcasted_iota(jnp.int32, shape, 0) * 1024
            + lax.broadcasted_iota(jnp.int32, shape, 1) * 128
            + lax.broadcasted_iota(jnp.int32, shape, 2)
        ) + (d * (K * lines) + i * piece) * 128
        block = jnp.zeros(shape, jnp.int32)
        scale = jnp.broadcast_to(factors[0][0][None], shape)
        inv = jnp.broadcast_to(factors[0][1][None], shape)
        for c in range(1, blocks):
            after = at >= ends[c - 1]
            block = jnp.where(after, c, block)
            scale = jnp.where(after, factors[c][0][None], scale)
            inv = jnp.where(after, factors[c][1][None], inv)
        rows = span(i, piece)
        block_buf[rows] = block.reshape(piece, 128)
        scale_buf[rows] = scale.reshape(piece, 128)
        inv_buf[rows] = inv.reshape(piece, 128)

    each(0, K * lines // piece, prepare)

    def phase(h, carry):
        dist = far - h

        def one(k, carry):
            relay(0, dist, k)
            relay(1, dist, k)
            return carry

        return lax.fori_loop(0, K, one, carry)

    if far > 2:
        lax.fori_loop(2, far - 1, phase, 0)

        def last_phase(k):
            end_relay(0, k)
            end_relay(1, k)

        each(0, K, last_phase)

    def stage_q(t):
        await_end(0, t)
        await_end(1, t)

        def step(i, tops):
            rows = pl.ds(pl.multiple_of(t * sub + i * piece, piece), piece)
            value = own[d, rows].astype(f32)
            value = value + ring[0, 0, rows].astype(f32) + ring[1, 0, rows].astype(f32)
            quant = jnp.clip(value * scale_buf[rows], -SATURATE, SATURATE)
            qown[rows] = quant.astype(bf)
            size = jnp.abs(value).reshape(piece // 8, 8, 128)
            block = block_buf[rows].reshape(piece // 8, 8, 128)
            return tuple(
                jnp.maximum(tops[c], jnp.max(jnp.where(block == c, size, 0.0), axis=0))
                for c in range(blocks)
            )

        tops = lax.fori_loop(0, sub // piece, step, tuple(acc[c] for c in range(blocks)))

        @pl.when(t < T - D)
        def _():
            q_copy(t).start()

        @pl.when(t >= T - D)
        def _():
            qall[t - (T - D), g] = qown[span(t, sub)]
            for j in range(1, grp):
                d_copy(t, j).start()

        for c in range(blocks):
            acc[c] = tops[c]

    def stage_pair(t):
        q_copy(t).wait_recv()
        pair[t, x] = (qown[mine(t)].astype(f32) + qsib[t].astype(f32)).astype(bf)
        for j in range(1, X):
            x_copy(t, j).start()

    def stage_mean(t):
        for j in range(1, X):
            x_arrival(t, j).wait_recv()
        value = pair[t, 0].astype(f32)
        for j in range(1, X):
            value = value + pair[t, j].astype(f32)
        mean = (value * inv_buf[mine(t)]).astype(bf)
        out[mine(t)] = mean
        fin_out[t] = mean
        f_copy(t).start()

    def stage_back(t):
        f_copy(t).wait_recv()
        out[theirs(t)] = fin_in[t]

    def stage_direct(t):
        for j in range(1, grp):
            d_arrival(t, j).wait_recv()
        i = t - (T - D)
        value = qall[i, 0].astype(f32)
        for j in range(1, grp):
            value = value + qall[i, j].astype(f32)
        rows = span(t, sub)
        out[rows] = (value * inv_buf[rows]).astype(bf)

    def stage_max():
        top = jnp.max(acc[...], axis=1)
        top = jnp.max(top, axis=1, keepdims=True)
        lane = lax.broadcasted_iota(jnp.int32, (blocks, 128), 1)
        row = lax.broadcasted_iota(jnp.int32, (blocks, 128), 0)
        msg[...] = jnp.max(jnp.where(lane == row, top, 0.0), axis=0, keepdims=True)
        each(0, devices - 1, lambda j: m_copy(j).start())

    def tick(t, carry):
        @pl.when(t < T)
        def _():
            stage_q(t)

        @pl.when(t == T - 1)
        def _():
            stage_max()

        @pl.when((t >= LAG_PAIR) & (t < T - D + LAG_PAIR))
        def _():
            stage_pair(t - LAG_PAIR)

        @pl.when((t >= LAG_MEAN) & (t < T - D + LAG_MEAN))
        def _():
            stage_mean(t - LAG_MEAN)

        @pl.when(t >= LAG_BACK)
        def _():
            stage_back(t - LAG_BACK)

        return carry

    lax.fori_loop(0, T - D + LAG_BACK, tick, 0)
    each(0, K, lambda k: drain(own.at[pl.ds(0, N - 1), span(k, lines)], r_send.at[k]))
    for t in range(T - D, T):
        stage_direct(t)

    drain(qsib, q_send)
    drain(fin_in, f_send)
    for j in range(1, X):
        drain(qsib, x_send)
    for j in range(1, grp):
        drain(qall.at[:, 0], d_send)
    drain(maxima, m_recv)
    top = jnp.maximum(jnp.max(maxima[...], axis=0), msg[...])
    amax_out[...] = top[0, :blocks].astype(bf)
    drain(maxima, m_send)


def put_out(mean, top, mean_out, top_out, sem):
    copies = [
        pltpu.make_async_copy(mean, mean_out, sem.at[0]),
        pltpu.make_async_copy(top, top_out, sem.at[1]),
    ]
    for copy in copies:
        copy.start()
    for copy in copies:
        copy.wait()


def body(gradients, block_len, amax_history):
    dp = lax.axis_size("dp")
    grp = lax.axis_size("grp")
    rows, lanes = gradients.shape[2:]
    own_rows = rows // dp
    Y = y_extent(dp)
    Z = dp // Y
    S, D = SPLIT, DIRECT
    K = min(CHUNKS, own_rows // (32 * S))
    T = K * S
    lines = own_rows // K
    sub = lines // S
    half = sub // CORES
    piece = min(32, sub)
    far = dp // 2
    X = grp // CORES
    blocks = block_len.shape[0]
    cfg = (dp, grp, Y, Z, K, S, D, lines, piece)
    bf, f32 = jnp.bfloat16, jnp.float32
    dma = pltpu.SemaphoreType.DMA
    part = (half, lanes)
    scratch = [
        pltpu.SMEM(block_len.shape, jnp.int32),
        pltpu.SMEM(amax_history.shape, f32),
        pltpu.VMEM((dp, own_rows, lanes), bf),
        pltpu.VMEM((2, far, own_rows, lanes), bf),
        pltpu.VMEM((own_rows, lanes), bf),
        pltpu.VMEM((T - D,) + part, bf),
        pltpu.VMEM((T - D, X) + part, bf),
        pltpu.VMEM((D, grp, sub, lanes), bf),
        pltpu.VMEM((T - D,) + part, bf),
        pltpu.VMEM((T - D,) + part, bf),
        pltpu.VMEM((own_rows, lanes), f32),
        pltpu.VMEM((own_rows, lanes), f32),
        pltpu.VMEM((own_rows, lanes), jnp.int32),
        pltpu.VMEM((blocks, 8, lanes), f32),
        pltpu.VMEM((1, lanes), f32),
        pltpu.VMEM((dp * grp - 1, 1, lanes), f32),
        dma((2,)),
        dma((dp,)),
        dma((K,)), dma((2, far, K)), dma((2, T)),
        dma(()), dma((T - D,)),
        dma(()), dma((T - D, X - 1)),
        dma(()), dma((T - D,)),
        dma(()), dma((D, grp - 1)),
        dma(()), dma(()),
    ]
    hbm = pl.BlockSpec(memory_space=pltpu.HBM)
    vmem = pl.BlockSpec(memory_space=pltpu.VMEM)
    anywhere = pl.BlockSpec(memory_space=pl.ANY)
    pinned = [
        pltpu.with_memory_space_constraint(a, pltpu.HBM)
        for a in (block_len, amax_history, gradients.reshape((dp, own_rows, lanes)))
    ]
    shapes = (
        jax.ShapeDtypeStruct((own_rows, lanes), bf),
        jax.ShapeDtypeStruct((blocks,), bf),
    )
    mean, top = pl.pallas_call(
        functools.partial(kernel, cfg),
        out_shape=shapes,
        in_specs=[hbm, hbm, hbm],
        out_specs=(vmem, vmem),
        scratch_shapes=scratch,
        compiler_params=pltpu.CompilerParams(
            collective_id=0, has_side_effects=True, vmem_limit_bytes=24 << 20
        ),
    )(*pinned)
    return pl.pallas_call(
        put_out,
        out_shape=shapes,
        in_specs=[anywhere, anywhere],
        out_specs=(hbm, hbm),
        scratch_shapes=[dma((2,))],
        compiler_params=pltpu.CompilerParams(vmem_limit_bytes=24 << 20),
    )(mean, top)


def solution(mesh):
    placed = (P("grp", "dp", None, None), P(), P())
    return jax.shard_map(
        body, mesh=mesh, in_specs=placed, out_specs=(P("dp", None), P()), check_vma=False
    )
```

time: 56.1 us -> 53.7 us (0.957)
  local copies, waits for them, and re-layouts: 1.31 us -> 0 us
  Pallas kernels: 54 us -> 52.9 us
    pallas_call x1 -> x2, Pallas kernels: 54 us -> 52.9 us  [the longest x1 52.1 us: body(): pl.pallas_call(functools.partial(kernel, cfg), out_shape=shapes, in_specs...]
    unnamed x1 -> x0, local copies, waits for them, and re-layouts: 0.79 us -> none
where the time goes in v2:
time: 53.7 us; the launch traced here: 53.5 us
  Pallas kernels  52.9 us (99%)
  between operations  0.64 us (1%)
    pallas_call x1, Pallas kernels, body(): pl.pallas_call(functools.partial(kernel, cfg), out_shape=shapes, in_specs...  52.1 us

profile of v2, /device:TPU:0, one launch (start us, length us, event | category | flops | bytes accessed | tf_op | source)
XLA Modules:
  0.0 53.5 jit_solution(13614708337287056264)
XLA Ops:
  0.6 52.1 %shard_map.50 = (bf16[2048,128]{1,0:T(8,128)(2,1)S(1)}, bf16[16]{0:T(256)(128)(2,1)S(1)}) custom-call(s32[16]{0:T(128)} %len_hbm.1, f32[4,16]{1,0:T(4,128)} %hist_hbm.1, bf16[8,2048,128]{2,1,0:T(8,128)(2,1)} %bitcast.1), custom_call_target="tpu_custom_call" | custom-call | tf_op jit(solution)/shard_map/pallas_call | solution.py:450
  52.7 0.8 %shard_map.51 = (bf16[2048,128]{1,0:T(8,128)(2,1)}, bf16[16]{0:T(256)(128)(2,1)}) custom-call(bf16[2048,128]{1,0:T(8,128)(2,1)S(1)} %get-tuple-element.4.mean, bf16[16]{0:T(256)(128)(2,1)S(1)} %get-tuple-element.5.top), custom_call_target="tpu_custom_call" | custom-call | tf_op jit(solution)/shard_map/pallas_call | solution.py:460

commit v3 on v2

--- a/solution.py
+++ b/solution.py
@@ -11,6 +11,7 @@
 CHUNKS = 4
 SPLIT = 4
 DIRECT = 1
+SHARED = 2
 CORES = 2
 LAG_PAIR = 2
 LAG_MEAN = 7
@@ -27,16 +28,17 @@
 
 def kernel(
     cfg, len_hbm, hist_hbm, grad, out, amax_out,
-    len_ref, hist_ref, own, ring, qown, qsib, pair, qall, fin_out, fin_in,
+    len_ref, hist_ref, own, ring, qown, qsib, pair, qall, pall, fin_out, fin_in,
     scale_buf, inv_buf, block_buf, acc, msg, maxima,
     small_sem, own_sem, r_send, r_recv, e_recv, q_send, q_recv, x_send, x_recv,
-    f_send, f_recv, d_send, d_recv, m_send, m_recv,
+    f_send, f_recv, d_send, d_recv, p_send, p_recv, m_send, m_recv,
 ):
-    N, grp, Y, Z, K, S, D, lines, piece = cfg
+    N, grp, Y, Z, K, S, D, E, lines, piece = cfg
     far = N // 2
     X = grp // CORES
     sub = lines // S
     T = K * S
+    Q = T - D - E
     half = sub // CORES
     blocks = len_ref.shape[0]
     hist = hist_ref.shape[0]
@@ -165,12 +167,28 @@
         here = qall.at[i, (g + grp - j) % grp]
         return remote(here, here, d_send, d_recv.at[i, j - 1], peer(grp - j))
 
-    def m_copy(j):
-        flat = d * grp + g
-        to = j + (j - flat + devices) // devices
-        slot = flat - (flat - to - 1 + devices) // devices
-        return remote(msg, maxima.at[slot], m_send, m_recv,
-                      {"dp": to // grp, "grp": to % grp})
+    def p_copy(t, j):
+        here = pall.at[t - Q, core, x]
+        return remote(here, here, p_send, p_recv.at[t - Q, j - 1], peer(j))
+
+    def p_arrival(t, j):
+        other = (g + grp - j) % grp
+        here = pall.at[t - Q, other % CORES, other // CORES]
+        return remote(here, here, p_send, p_recv.at[t - Q, j - 1], peer(grp - j))
+
+    def m_copy(i, j):
+        return remote(msg, maxima.at[i * grp + j - 1], m_send, m_recv,
+                      {"dp": (d + i) % N, "grp": (g + j) % grp})
+
+    def send_max():
+        for j in range(1, grp):
+            m_copy(0, j).start()
+
+        def one(i):
+            for j in range(grp):
+                m_copy(i, j).start()
+
+        each(1, N, one)
 
     def drain(ref, sem):
         pltpu.make_async_copy(ref, ref, sem).wait()
@@ -301,9 +319,19 @@
 
     def stage_pair(t):
         q_copy(t).wait_recv()
-        pair[t, x] = (qown[mine(t)].astype(f32) + qsib[t].astype(f32)).astype(bf)
-        for j in range(1, X):
-            x_copy(t, j).start()
+        both = (qown[mine(t)].astype(f32) + qsib[t].astype(f32)).astype(bf)
+
+        @pl.when(t < Q)
+        def _():
+            pair[t, x] = both
+            for j in range(1, X):
+                x_copy(t, j).start()
+
+        @pl.when(t >= Q)
+        def _():
+            pall[t - Q, core, x] = both
+            for j in range(1, grp):
+                p_copy(t, j).start()
 
     def stage_mean(t):
         for j in range(1, X):
@@ -320,6 +348,16 @@
         f_copy(t).wait_recv()
         out[theirs(t)] = fin_in[t]
 
+    def stage_shared(t):
+        for j in range(1, grp):
+            p_arrival(t, j).wait_recv()
+        for c in range(CORES):
+            value = pall[t - Q, c, 0].astype(f32)
+            for j in range(1, X):
+                value = value + pall[t - Q, c, j].astype(f32)
+            rows = pl.ds(pl.multiple_of(t * sub + c * half, half), half)
+            out[rows] = (value * inv_buf[rows]).astype(bf)
+
     def stage_direct(t):
         for j in range(1, grp):
             d_arrival(t, j).wait_recv()
@@ -336,7 +374,7 @@
         lane = lax.broadcasted_iota(jnp.int32, (blocks, 128), 1)
         row = lax.broadcasted_iota(jnp.int32, (blocks, 128), 0)
         msg[...] = jnp.max(jnp.where(lane == row, top, 0.0), axis=0, keepdims=True)
-        each(0, devices - 1, lambda j: m_copy(j).start())
+        send_max()
 
     def tick(t, carry):
         @pl.when(t < T)
@@ -351,27 +389,30 @@
         def _():
             stage_pair(t - LAG_PAIR)
 
-        @pl.when((t >= LAG_MEAN) & (t < T - D + LAG_MEAN))
+        @pl.when((t >= LAG_MEAN) & (t < Q + LAG_MEAN))
         def _():
             stage_mean(t - LAG_MEAN)
 
-        @pl.when(t >= LAG_BACK)
+        @pl.when((t >= LAG_BACK) & (t < Q + LAG_BACK))
         def _():
             stage_back(t - LAG_BACK)
 
         return carry
 
-    lax.fori_loop(0, T - D + LAG_BACK, tick, 0)
+    lax.fori_loop(0, max(Q + LAG_BACK, T - D + LAG_PAIR), tick, 0)
     each(0, K, lambda k: drain(own.at[pl.ds(0, N - 1), span(k, lines)], r_send.at[k]))
+    for t in range(Q, T - D):
+        stage_shared(t)
     for t in range(T - D, T):
         stage_direct(t)
 
     drain(qsib, q_send)
     drain(fin_in, f_send)
     for j in range(1, X):
-        drain(qsib, x_send)
+        drain(fin_in, x_send)
     for j in range(1, grp):
         drain(qall.at[:, 0], d_send)
+        drain(pall.at[:, 0, 0], p_send)
     drain(maxima, m_recv)
     top = jnp.maximum(jnp.max(maxima[...], axis=0), msg[...])
     amax_out[...] = top[0, :blocks].astype(bf)
@@ -396,17 +437,18 @@
     own_rows = rows // dp
     Y = y_extent(dp)
     Z = dp // Y
-    S, D = SPLIT, DIRECT
+    S, D, E = SPLIT, DIRECT, SHARED
     K = min(CHUNKS, own_rows // (32 * S))
     T = K * S
     lines = own_rows // K
     sub = lines // S
     half = sub // CORES
-    piece = min(32, sub)
+    piece = min(64, sub)
     far = dp // 2
     X = grp // CORES
     blocks = block_len.shape[0]
-    cfg = (dp, grp, Y, Z, K, S, D, lines, piece)
+    Q = T - D - E
+    cfg = (dp, grp, Y, Z, K, S, D, E, lines, piece)
     bf, f32 = jnp.bfloat16, jnp.float32
     dma = pltpu.SemaphoreType.DMA
     part = (half, lanes)
@@ -417,10 +459,11 @@
         pltpu.VMEM((2, far, own_rows, lanes), bf),
         pltpu.VMEM((own_rows, lanes), bf),
         pltpu.VMEM((T - D,) + part, bf),
-        pltpu.VMEM((T - D, X) + part, bf),
+        pltpu.VMEM((Q, X) + part, bf),
         pltpu.VMEM((D, grp, sub, lanes), bf),
-        pltpu.VMEM((T - D,) + part, bf),
-        pltpu.VMEM((T - D,) + part, bf),
+        pltpu.VMEM((E, CORES, X) + part, bf),
+        pltpu.VMEM((Q,) + part, bf),
+        pltpu.VMEM((Q,) + part, bf),
         pltpu.VMEM((own_rows, lanes), f32),
         pltpu.VMEM((own_rows, lanes), f32),
         pltpu.VMEM((own_rows, lanes), jnp.int32),
@@ -431,9 +474,10 @@
         dma((dp,)),
         dma((K,)), dma((2, far, K)), dma((2, T)),
         dma(()), dma((T - D,)),
-        dma(()), dma((T - D, X - 1)),
-        dma(()), dma((T - D,)),
+        dma(()), dma((Q, X - 1)),
+        dma(()), dma((Q,)),
         dma(()), dma((D, grp - 1)),
+        dma(()), dma((E, grp - 1)),
         dma(()), dma(()),
     ]
     hbm = pl.BlockSpec(memory_space=pltpu.HBM)

time: 53.7 us -> 53.7 us (level)
  no operation moved by 1% of the time
where the time goes in v3:
time: 53.7 us; the launch traced here: 53.5 us
  Pallas kernels  52.9 us (99%)
  between operations  0.64 us (1%)
    pallas_call x1, Pallas kernels, body(): pl.pallas_call(functools.partial(kernel, cfg), out_shape=shapes, in_specs...  52.1 us

profile of v3, /device:TPU:0, one launch (start us, length us, event | category | flops | bytes accessed | tf_op | source)
XLA Modules:
  0.0 53.5 jit_solution(13023646307875557542)
XLA Ops:
  0.6 52.1 %shard_map.50 = (bf16[2048,128]{1,0:T(8,128)(2,1)S(1)}, bf16[16]{0:T(256)(128)(2,1)S(1)}) custom-call(s32[16]{0:T(128)} %len_hbm.1, f32[4,16]{1,0:T(4,128)} %hist_hbm.1, bf16[8,2048,128]{2,1,0:T(8,128)(2,1)} %bitcast.1), custom_call_target="tpu_custom_call" | custom-call | tf_op jit(solution)/shard_map/pallas_call | solution.py:494
  52.7 0.8 %shard_map.51 = (bf16[2048,128]{1,0:T(8,128)(2,1)}, bf16[16]{0:T(256)(128)(2,1)}) custom-call(bf16[2048,128]{1,0:T(8,128)(2,1)S(1)} %get-tuple-element.4.mean, bf16[16]{0:T(256)(128)(2,1)S(1)} %get-tuple-element.5.top), custom_call_target="tpu_custom_call" | custom-call | tf_op jit(solution)/shard_map/pallas_call | solution.py:504

commit v4 on v3

--- a/solution.py
+++ b/solution.py
@@ -16,6 +16,7 @@
 LAG_PAIR = 2
 LAG_MEAN = 7
 LAG_BACK = 9
+HELD = 4
 MESH = pl.DeviceIdType.MESH
 
 
@@ -176,19 +177,17 @@
         here = pall.at[t - Q, other % CORES, other // CORES]
         return remote(here, here, p_send, p_recv.at[t - Q, j - 1], peer(grp - j))
 
-    def m_copy(i, j):
-        return remote(msg, maxima.at[i * grp + j - 1], m_send, m_recv,
-                      {"dp": (d + i) % N, "grp": (g + j) % grp})
-
     def send_max():
-        for j in range(1, grp):
-            m_copy(0, j).start()
+        flat = d * grp + g
+        maxima[flat] = msg[...]
 
         def one(i):
             for j in range(grp):
-                m_copy(i, j).start()
-
-        each(1, N, one)
+                @pl.when((i != d) | (j != g))
+                def _(j=j):
+                    remote(msg, maxima.at[flat], m_send, m_recv, {"dp": i, "grp": j}).start()
+
+        each(0, N, one)
 
     def drain(ref, sem):
         pltpu.make_async_copy(ref, ref, sem).wait()
@@ -283,7 +282,11 @@
             end_relay(0, k)
             end_relay(1, k)
 
-        each(0, K, last_phase)
+        each(0, K - 1, last_phase)
+
+        @pl.when(core == 0)
+        def _():
+            last_phase(K - 1)
 
     def stage_q(t):
         await_end(0, t)
@@ -377,6 +380,12 @@
         send_max()
 
     def tick(t, carry):
+        if far > 2:
+            @pl.when((t == max((K - 1) * S - HELD, 0)) & (core > 0))
+            def _():
+                end_relay(0, K - 1)
+                end_relay(1, K - 1)
+
         @pl.when(t < T)
         def _():
             stage_q(t)
@@ -413,10 +422,10 @@
     for j in range(1, grp):
         drain(qall.at[:, 0], d_send)
         drain(pall.at[:, 0, 0], p_send)
-    drain(maxima, m_recv)
-    top = jnp.maximum(jnp.max(maxima[...], axis=0), msg[...])
+    drain(maxima.at[pl.ds(0, devices - 1)], m_recv)
+    top = jnp.max(maxima[...], axis=0)
     amax_out[...] = top[0, :blocks].astype(bf)
-    drain(maxima, m_send)
+    drain(maxima.at[pl.ds(0, devices - 1)], m_send)
 
 
 def put_out(mean, top, mean_out, top_out, sem):
@@ -469,7 +478,7 @@
         pltpu.VMEM((own_rows, lanes), jnp.int32),
         pltpu.VMEM((blocks, 8, lanes), f32),
         pltpu.VMEM((1, lanes), f32),
-        pltpu.VMEM((dp * grp - 1, 1, lanes), f32),
+        pltpu.VMEM((dp * grp, 1, lanes), f32),
         dma((2,)),
         dma((dp,)),
         dma((K,)), dma((2, far, K)), dma((2, T)),

time: 53.7 us -> 53.5 us (level)
  no operation moved by 1% of the time
where the time goes in v4:
time: 53.5 us; the launch traced here: 53.4 us
  Pallas kernels  52.7 us (99%)
  between operations  0.64 us (1%)
    pallas_call x1, Pallas kernels, body(): pl.pallas_call(functools.partial(kernel, cfg), out_shape=shapes, in_specs...  51.9 us

profile of v4, /device:TPU:0, one launch (start us, length us, event | category | flops | bytes accessed | tf_op | source)
XLA Modules:
  0.0 53.4 jit_solution(13808270856907879009)
XLA Ops:
  0.6 51.9 %shard_map.50 = (bf16[2048,128]{1,0:T(8,128)(2,1)S(1)}, bf16[16]{0:T(256)(128)(2,1)S(1)}) custom-call(s32[16]{0:T(128)} %len_hbm.1, f32[4,16]{1,0:T(4,128)} %hist_hbm.1, bf16[8,2048,128]{2,1,0:T(8,128)(2,1)} %bitcast.1), custom_call_target="tpu_custom_call" | custom-call | tf_op jit(solution)/shard_map/pallas_call | solution.py:503
  52.6 0.8 %shard_map.51 = (bf16[2048,128]{1,0:T(8,128)(2,1)}, bf16[16]{0:T(256)(128)(2,1)}) custom-call(bf16[2048,128]{1,0:T(8,128)(2,1)S(1)} %get-tuple-element.4.mean, bf16[16]{0:T(256)(128)(2,1)S(1)} %get-tuple-element.5.top), custom_call_target="tpu_custom_call" | custom-call | tf_op jit(solution)/shard_map/pallas_call | solution.py:513
